TPU v7x, 32 devices: a whole 2x2x4 slice. The times are simulated.
32 devices in a mesh: cohort: 2 (over x), tile: 16 (over z, y, core).
Axes of the slice: x: 2, y: 2, z: 4, core: 2. Of those that a mesh axis runs over, the one named last changes fastest.
Arguments:
- dosage: bfloat16 [512, 8192], P(('cohort', 'tile')), parts along dimension 0, may hold values from 0 to 2
- covars: float32 [512, 16], P(('cohort', 'tile')), parts along dimension 0, may hold values from -12 to 12, as said below
- phenotypes: float32 [512, 1792], P(('cohort', 'tile')), parts along dimension 0, may hold values from -100 to 100
Outputs:
- mean_chi: float32 [3584], P(('cohort', 'tile')), parts along dimension 0
- hit_rate: float32 [3584], P(('cohort', 'tile')), parts along dimension 0
There are 2 independent parts, one for each index of `cohort`. A program takes and returns all parts, laid end to end along the dimension named above; each array names one. Nothing has to cross between parts.
Inputs may be any that keep to these rules, and one draw needn't show every extreme that they name: `covars`: each covariate column has its own mean and spread.
All inputs are finite; a program needn't handle non-finite values.
Results may differ from a plain program's by a relative error of at most 0.003.
Values may be sent and summed in bfloat16 or wider, within the bound.
A program may use at most 64 MiB of HBM per device.

v0:
```python
import jax
import jax.numpy as jnp
from jax import lax
from jax.sharding import PartitionSpec as P


def local(dosage, covars, phenotypes):
    highest = lax.Precision.HIGHEST
    devices = lax.axis_size("tile")
    local_rows = dosage.shape[0]
    variants = dosage.shape[1]
    samples = local_rows * devices
    genes_all = phenotypes.shape[1]
    gene_own = genes_all // devices
    scale_root = jnp.sqrt(jnp.float32(samples))
    covars_all = lax.all_gather(covars, "tile", axis=0, tiled=True)
    dose_all = lax.all_gather(dosage, "tile", axis=0, tiled=True)
    pheno_own = lax.all_to_all(phenotypes, "tile", split_axis=1, concat_axis=0, tiled=True)
    gram = jnp.dot(covars_all.T, covars_all, precision=highest, preferred_element_type=jnp.float32)
    factor = jnp.linalg.cholesky(gram)
    cov_pheno = jnp.dot(
        covars_all.T, pheno_own, precision=highest, preferred_element_type=jnp.float32
    )
    beta_pheno = jax.scipy.linalg.cho_solve((factor, True), cov_pheno)
    pheno_resid = pheno_own - jnp.dot(
        covars_all, beta_pheno, precision=highest, preferred_element_type=jnp.float32
    )
    pheno_sumsq = jnp.sum(pheno_resid * pheno_resid, axis=0)
    pheno_bf = pheno_resid.astype(jnp.bfloat16)
    pheno_var = pheno_sumsq / samples + 0.1
    width = 1024
    blocks = variants // width

    def one_block(index, totals):
        start = index * width
        dose_block = lax.dynamic_slice_in_dim(dose_all, start, width, 1).astype(jnp.float32)
        cov_dose = jnp.dot(
            covars_all.T, dose_block, precision=highest, preferred_element_type=jnp.float32
        )
        beta_dose = jax.scipy.linalg.cho_solve((factor, True), cov_dose)
        dose_resid = dose_block - jnp.dot(
            covars_all, beta_dose, precision=highest, preferred_element_type=jnp.float32
        )
        dose_var = jnp.sum(dose_resid * dose_resid, axis=0) / samples + 0.1
        cross = lax.dot_general(
            pheno_bf,
            dose_resid.astype(jnp.bfloat16),
            (((0,), (0,)), ((), ())),
            preferred_element_type=jnp.float32,
        )
        zscore = cross / (scale_root * jnp.sqrt(pheno_var[:, None] * dose_var[None, :]))
        chi_square = zscore * zscore
        return (
            totals[0] + jnp.sum(chi_square, axis=1),
            totals[1] + jnp.sum(jax.nn.sigmoid(2.0 * (chi_square - 4.0)), axis=1),
        )

    zeros = jnp.zeros((gene_own,), jnp.float32)
    chi_total, hit_total = lax.fori_loop(0, blocks, one_block, (zeros, zeros))
    return (chi_total / variants, 20.0 / variants * hit_total)


def solution(mesh):
    return jax.shard_map(
        local,
        mesh=mesh,
        in_specs=(
            P(("cohort", "tile"), None),
            P(("cohort", "tile"), None),
            P(("cohort", "tile"), None),
        ),
        out_specs=(P(("cohort", "tile")), P(("cohort", "tile"))),
        check_vma=False,
    )
```

profile of v0, /device:TPU:0, one launch (start us, length us, event | category | flops | bytes accessed | tf_op | source)
XLA Modules:
  0.0 117.5 jit_solution(11533161251048784845)
XLA Ops:
  9.6 7.4 %all-to-all-start = ((f32[16,16,112]{2,0,1:T(8,128)}), f32[16,16,112]{2,0,1:T(8,128)S(1)}, u32[]{:S(2)}, u32[]{:S(2)}) async-start(f32[16,16,112]{2,0,1:T(8,128)} %copy.15), calls=%async_computation | async-start | bytes 262144 | tf_op jit(solution)/shard_map/all_to_all | solution.py:18
  17.0 22.7 %all_gather.7 = f32[256,16]{1,0:T(8,128)S(1)} all-gather(f32[16,16]{1,0:T(8,128)} %param.6), channel_id=1, replica_groups=mesh['cohort'=2,'tile'=16] {'tile'}, dimensions={0}, use_global_device_ids=true | all-gather | bytes 17408 | tf_op jit(solution)/shard_map/all_gather | solution.py:16
  40.2 1.5 %cholesky.18 = f32[16,16]{1,0:T(8,128)S(1)} custom-call(f32[16,16]{1,0:T(8,128)S(1)} %fusion.19), custom_call_target="Cholesky" | custom-call | tf_op jit(solution)/shard_map/jit(cholesky)/cholesky | solution.py:20
  43.0 1.2 %custom-call.24 = f32[1,16,16]{1,2,0:T(8,128)S(1)} custom-call(f32[1,16,16]{2,1,0:T(8,128)S(1)} %get-tuple-element.272), custom_call_target="InvertDiagBlocksLowerTriangular" | custom-call | tf_op jit(solution)/shard_map/jit(_cho_solve)/triangular_solve | solution.py:24
  45.6 18.0 %all-gather.2.cloned.1.call-done = bf16[256,8192]{1,0:T(8,128)(2,1)} async-done(((bf16[16,8192]{1,0:T(8,128)(2,1)}), bf16[256,8192]{1,0:T(8,128)(2,1)}) %all-gather.2.cloned.1.call-update) | async-done | bytes 4194320 | tf_op jit(solution)/shard_map/all_gather | solution.py:17
  63.6 46.5 %while.18 = (s32[]{:T(128)}, f32[112]{0:T(128)S(1)}, f32[112]{0:T(128)S(1)}, bf16[256,8192]{1,0:T(8,128)(2,1)}, f32[16,16]{1,0:T(8,128)S(1)}, /*index=5*/f32[256...) while((s32[]{:T(128)}, f32[112]{0:T(128)S(1)}, ...), condition=%wide.region_7.8_spmd.clone, body=%wide.region_3.7_spmd.clone.sunk | while | flops 168249056 | bytes 2605173 | solution.py:59
  63.6 1.4 %fusion.62 = f32[1024,16]{0,1:T(8,128)S(1)} fusion(f32[256,16]{0,1:T(8,128)S(1)} %get-tuple-element.375, bf16[256,8192]{1,0:T(8,128)(2,1)} %get-tuple-element.373, s32[]{:T(128)S(6)} %select_n.19), kind=kOutput, calls=%fused_computation.7.clone.1 | convolution fusion | flops 50331648 | bytes 606212 | tf_op jit(solution)/shard_map/while/body/eval_jaxpr/dot_general | solution.py:37
  65.0 1.2 %custom-call.29 = f32[1,16,16]{1,2,0:T(8,128)S(1)} custom-call(f32[1,16,16]{2,1,0:T(8,128)S(1)} %bitcast_select_fusion.2), custom_call_target="InvertDiagBlocksLowerTriangular" | custom-call | tf_op jit(solution)/shard_map/while/body/eval_jaxpr/jit(_cho_solve)/triangular_solve | solution.py:40
  66.7 2.1 %multiply_reduce_fusion.3 = (f32[1024]{0:T(1024)S(1)}, bf16[256,1024]{1,0:T(8,128)(2,1)S(1)}) fusion(f32[16,1024]{1,0:T(8,128)S(1)} %fusion.64, f32[256,16]{0,1:T(8,128)S(1)} %get-tuple-element.375, bf16[256,8192]{1,0:T(8,128)(2,1)} %get-tuple-element.373, s32[]{:T(128)S(6)} %select_n.19), kind=kOutput, calls=%fused_computation.5.clone.1 | convolution fusion | flops 51641344 | bytes 1134596 | tf_op jit(solution)/shard_map/while/body/eval_jaxpr/dot_general | solution.py:41
  69.4 1.4 %fusion.62 = f32[1024,16]{0,1:T(8,128)S(1)} fusion(f32[256,16]{0,1:T(8,128)S(1)} %get-tuple-element.375, bf16[256,8192]{1,0:T(8,128)(2,1)} %get-tuple-element.373, s32[]{:T(128)S(6)} %select_n.19), kind=kOutput, calls=%fused_computation.7.clone.1 | convolution fusion | flops 50331648 | bytes 606212 | tf_op jit(solution)/shard_map/while/body/eval_jaxpr/dot_general | solution.py:37
  72.5 2.1 %multiply_reduce_fusion.3 = (f32[1024]{0:T(1024)S(1)}, bf16[256,1024]{1,0:T(8,128)(2,1)S(1)}) fusion(f32[16,1024]{1,0:T(8,128)S(1)} %fusion.64, f32[256,16]{0,1:T(8,128)S(1)} %get-tuple-element.375, bf16[256,8192]{1,0:T(8,128)(2,1)} %get-tuple-element.373, s32[]{:T(128)S(6)} %select_n.19), kind=kOutput, calls=%fused_computation.5.clone.1 | convolution fusion | flops 51641344 | bytes 1134596 | tf_op jit(solution)/shard_map/while/body/eval_jaxpr/dot_general | solution.py:41
  75.2 1.4 %fusion.62 = f32[1024,16]{0,1:T(8,128)S(1)} fusion(f32[256,16]{0,1:T(8,128)S(1)} %get-tuple-element.375, bf16[256,8192]{1,0:T(8,128)(2,1)} %get-tuple-element.373, s32[]{:T(128)S(6)} %select_n.19), kind=kOutput, calls=%fused_computation.7.clone.1 | convolution fusion | flops 50331648 | bytes 606212 | tf_op jit(solution)/shard_map/while/body/eval_jaxpr/dot_general | solution.py:37
  78.3 2.1 %multiply_reduce_fusion.3 = (f32[1024]{0:T(1024)S(1)}, bf16[256,1024]{1,0:T(8,128)(2,1)S(1)}) fusion(f32[16,1024]{1,0:T(8,128)S(1)} %fusion.64, f32[256,16]{0,1:T(8,128)S(1)} %get-tuple-element.375, bf16[256,8192]{1,0:T(8,128)(2,1)} %get-tuple-element.373, s32[]{:T(128)S(6)} %select_n.19), kind=kOutput, calls=%fused_computation.5.clone.1 | convolution fusion | flops 51641344 | bytes 1134596 | tf_op jit(solution)/shard_map/while/body/eval_jaxpr/dot_general | solution.py:41
  81.1 1.4 %fusion.62 = f32[1024,16]{0,1:T(8,128)S(1)} fusion(f32[256,16]{0,1:T(8,128)S(1)} %get-tuple-element.375, bf16[256,8192]{1,0:T(8,128)(2,1)} %get-tuple-element.373, s32[]{:T(128)S(6)} %select_n.19), kind=kOutput, calls=%fused_computation.7.clone.1 | convolution fusion | flops 50331648 | bytes 606212 | tf_op jit(solution)/shard_map/while/body/eval_jaxpr/dot_general | solution.py:37
  84.1 2.1 %multiply_reduce_fusion.3 = (f32[1024]{0:T(1024)S(1)}, bf16[256,1024]{1,0:T(8,128)(2,1)S(1)}) fusion(f32[16,1024]{1,0:T(8,128)S(1)} %fusion.64, f32[256,16]{0,1:T(8,128)S(1)} %get-tuple-element.375, bf16[256,8192]{1,0:T(8,128)(2,1)} %get-tuple-element.373, s32[]{:T(128)S(6)} %select_n.19), kind=kOutput, calls=%fused_computation.5.clone.1 | convolution fusion | flops 51641344 | bytes 1134596 | tf_op jit(solution)/shard_map/while/body/eval_jaxpr/dot_general | solution.py:41
  86.9 1.4 %fusion.62 = f32[1024,16]{0,1:T(8,128)S(1)} fusion(f32[256,16]{0,1:T(8,128)S(1)} %get-tuple-element.375, bf16[256,8192]{1,0:T(8,128)(2,1)} %get-tuple-element.373, s32[]{:T(128)S(6)} %select_n.19), kind=kOutput, calls=%fused_computation.7.clone.1 | convolution fusion | flops 50331648 | bytes 606212 | tf_op jit(solution)/shard_map/while/body/eval_jaxpr/dot_general | solution.py:37
  90.0 2.1 %multiply_reduce_fusion.3 = (f32[1024]{0:T(1024)S(1)}, bf16[256,1024]{1,0:T(8,128)(2,1)S(1)}) fusion(f32[16,1024]{1,0:T(8,128)S(1)} %fusion.64, f32[256,16]{0,1:T(8,128)S(1)} %get-tuple-element.375, bf16[256,8192]{1,0:T(8,128)(2,1)} %get-tuple-element.373, s32[]{:T(128)S(6)} %select_n.19), kind=kOutput, calls=%fused_computation.5.clone.1 | convolution fusion | flops 51641344 | bytes 1134596 | tf_op jit(solution)/shard_map/while/body/eval_jaxpr/dot_general | solution.py:41
  92.7 1.4 %fusion.62 = f32[1024,16]{0,1:T(8,128)S(1)} fusion(f32[256,16]{0,1:T(8,128)S(1)} %get-tuple-element.375, bf16[256,8192]{1,0:T(8,128)(2,1)} %get-tuple-element.373, s32[]{:T(128)S(6)} %select_n.19), kind=kOutput, calls=%fused_computation.7.clone.1 | convolution fusion | flops 50331648 | bytes 606212 | tf_op jit(solution)/shard_map/while/body/eval_jaxpr/dot_general | solution.py:37
  95.8 2.1 %multiply_reduce_fusion.3 = (f32[1024]{0:T(1024)S(1)}, bf16[256,1024]{1,0:T(8,128)(2,1)S(1)}) fusion(f32[16,1024]{1,0:T(8,128)S(1)} %fusion.64, f32[256,16]{0,1:T(8,128)S(1)} %get-tuple-element.375, bf16[256,8192]{1,0:T(8,128)(2,1)} %get-tuple-element.373, s32[]{:T(128)S(6)} %select_n.19), kind=kOutput, calls=%fused_computation.5.clone.1 | convolution fusion | flops 51641344 | bytes 1134596 | tf_op jit(solution)/shard_map/while/body/eval_jaxpr/dot_general | solution.py:41
  98.5 1.4 %fusion.62 = f32[1024,16]{0,1:T(8,128)S(1)} fusion(f32[256,16]{0,1:T(8,128)S(1)} %get-tuple-element.375, bf16[256,8192]{1,0:T(8,128)(2,1)} %get-tuple-element.373, s32[]{:T(128)S(6)} %select_n.19), kind=kOutput, calls=%fused_computation.7.clone.1 | convolution fusion | flops 50331648 | bytes 606212 | tf_op jit(solution)/shard_map/while/body/eval_jaxpr/dot_general | solution.py:37
  101.6 2.1 %multiply_reduce_fusion.3 = (f32[1024]{0:T(1024)S(1)}, bf16[256,1024]{1,0:T(8,128)(2,1)S(1)}) fusion(f32[16,1024]{1,0:T(8,128)S(1)} %fusion.64, f32[256,16]{0,1:T(8,128)S(1)} %get-tuple-element.375, bf16[256,8192]{1,0:T(8,128)(2,1)} %get-tuple-element.373, s32[]{:T(128)S(6)} %select_n.19), kind=kOutput, calls=%fused_computation.5.clone.1 | convolution fusion | flops 51641344 | bytes 1134596 | tf_op jit(solution)/shard_map/while/body/eval_jaxpr/dot_general | solution.py:41
  104.3 1.4 %fusion.62 = f32[1024,16]{0,1:T(8,128)S(1)} fusion(f32[256,16]{0,1:T(8,128)S(1)} %get-tuple-element.375, bf16[256,8192]{1,0:T(8,128)(2,1)} %get-tuple-element.373, s32[]{:T(128)S(6)} %select_n.19), kind=kOutput, calls=%fused_computation.7.clone.1 | convolution fusion | flops 50331648 | bytes 606212 | tf_op jit(solution)/shard_map/while/body/eval_jaxpr/dot_general | solution.py:37
  105.7 1.2 %custom-call.29 = f32[1,16,16]{1,2,0:T(8,128)S(1)} custom-call(f32[1,16,16]{2,1,0:T(8,128)S(1)} %bitcast_select_fusion.2), custom_call_target="InvertDiagBlocksLowerTriangular" | custom-call | tf_op jit(solution)/shard_map/while/body/eval_jaxpr/jit(_cho_solve)/triangular_solve | solution.py:40
  107.4 2.1 %multiply_reduce_fusion.3 = (f32[1024]{0:T(1024)S(1)}, bf16[256,1024]{1,0:T(8,128)(2,1)S(1)}) fusion(f32[16,1024]{1,0:T(8,128)S(1)} %fusion.64, f32[256,16]{0,1:T(8,128)S(1)} %get-tuple-element.375, bf16[256,8192]{1,0:T(8,128)(2,1)} %get-tuple-element.373, s32[]{:T(128)S(6)} %select_n.19), kind=kOutput, calls=%fused_computation.5.clone.1 | convolution fusion | flops 51641344 | bytes 1134596 | tf_op jit(solution)/shard_map/while/body/eval_jaxpr/dot_general | solution.py:41
  (76 shorter events, 21.8 us)
Async XLA Ops:
  7.2 56.5 %all-gather.2.cloned.1.call-start = ((), (), s32[]{:S(2)}) async-start(), calls=%async_computation.1 | async-start | bytes 4456448 | tf_op jit(solution)/shard_map/all_gather | solution.py:17
  9.6 34.7 %all-to-all-start = ((f32[16,16,112]{2,0,1:T(8,128)}), f32[16,16,112]{2,0,1:T(8,128)S(1)}, u32[]{:S(2)}, u32[]{:S(2)}) async-start(f32[16,16,112]{2,0,1:T(8,128)} %copy.15), calls=%async_computation | async-start | bytes 262144 | tf_op jit(solution)/shard_map/all_to_all | solution.py:18
Sparse Core Ops, SparseCore 0:
  10.1 53.4 all-gather.1
where the time goes:
time: 118 us; the launch traced here: 117 us
  matrix products  37.4 us (32%)
  blocking collectives  22.7 us (19%)
  waiting for transfers between devices  18.7 us (16%)
  other arithmetic  14.6 us (12%)
  between operations  14.1 us (12%)
  starting transfers between devices  7.45 us (6%)
  local copies, waits for them, and re-layouts  2.05 us (2%)
    all_gather x1, blocking collectives, local(): covars_all = lax.all_gather(covars, 'tile', axis=0, tiled=True)  22.7 us
    all_gather x1, waiting for transfers between devices, local(): dose_all = lax.all_gather(dosage, 'tile', axis=0, tiled=True)  18 us
    dot_general x8, matrix products, one_block(): jnp.dot(covars_all, beta_dose, precision=highest, preferred_element_type=...  17 us
    dot_general x8, matrix products, one_block(): jnp.dot(covars_all.T, dose_block, precision=highest, preferred_element_ty...  10.9 us
    another operation x16, other arithmetic, one_block(): beta_dose = jax.scipy.linalg.cho_solve((factor, True), cov_dose)  9.88 us
    all_to_all x1, starting transfers between devices, local(): lax.all_to_all(phenotypes, 'tile', split_axis=1, concat_axis=0, tiled=True)  7.41 us
    dot_general x8, matrix products, one_block(): lax.dot_general(pheno_bf, dose_resid.astype(jnp.bfloat16), (((0,), (0,)),...  4.42 us
    another operation x16, matrix products, one_block(): beta_dose = jax.scipy.linalg.cho_solve((factor, True), cov_dose)  3.7 us
  transfers between devices with their start and end apart: 2, of which 1 were waited for; matrix products, arithmetic and copies ran while one was open for 6% of the time, Pallas kernels for 0%

commit v1 on v0

--- a/solution.py
+++ b/solution.py
@@ -14,7 +14,12 @@
     gene_own = genes_all // devices
     scale_root = jnp.sqrt(jnp.float32(samples))
     covars_all = lax.all_gather(covars, "tile", axis=0, tiled=True)
-    dose_all = lax.all_gather(dosage, "tile", axis=0, tiled=True)
+    ring = [dosage]
+    for hop in range(15):
+        ring.append(lax.ppermute(ring[-1], "tile", [(dev, (dev + 1) % 16) for dev in range(16)]))
+    dose_all = jnp.roll(
+        jnp.concatenate(ring[::-1], axis=0), (lax.axis_index("tile") + 1) * ring[0].shape[0], axis=0
+    )
     pheno_own = lax.all_to_all(phenotypes, "tile", split_axis=1, concat_axis=0, tiled=True)
     gram = jnp.dot(covars_all.T, covars_all, precision=highest, preferred_element_type=jnp.float32)
     factor = jnp.linalg.cholesky(gram)

time: 118 us -> 211 us (1.79)
  waiting for transfers between devices: 18.7 us -> 114 us
  between operations: 14.1 us -> 0.97 us
  local copies, waits for them, and re-layouts: 2.05 us -> 12.5 us
    ppermute x0 -> x15, waiting for transfers between devices: none -> 114 us  [local(): lax.ppermute(ring[-1], 'tile', [(dev, (dev + 1) % 16) for dev in range(16)])]
    all_gather x1 -> x0, waiting for transfers between devices: 18 us -> none  [local(): dose_all = lax.all_gather(dosage, 'tile', axis=0, tiled=True)]
    unnamed x2 -> x39, local copies, waits for them, and re-layouts: 0.17 us -> 8.39 us
    dynamic_slice x0 -> x1, local copies, waits for them, and re-layouts: none -> 2.23 us  [local(): jnp.roll(jnp.concatenate(ring[::-1], axis=0), (lax.axis_index('tile') + 1...]
  transfers between devices with their start and end apart: 2 -> 16, of which waited for: 1 -> 14; matrix products, arithmetic and copies ran while one was open for 6% -> 4% of each run, Pallas kernels for 0% -> 0%
where the time goes in v1:
time: 211 us; the launch traced here: 210 us
  waiting for transfers between devices  114 us (54%)
  matrix products  38.7 us (18%)
  blocking collectives  22.3 us (11%)
  other arithmetic  14.5 us (7%)
  local copies, waits for them, and re-layouts  12.5 us (6%)
  starting transfers between devices  6.76 us (3%)
    ppermute x15, waiting for transfers between devices, local(): lax.ppermute(ring[-1], 'tile', [(dev, (dev + 1) % 16) for dev in range(16)])  114 us
    all_gather x1, blocking collectives, local(): covars_all = lax.all_gather(covars, 'tile', axis=0, tiled=True)  22.3 us
    dot_general x8, matrix products, one_block(): jnp.dot(covars_all, beta_dose, precision=highest, preferred_element_type=...  17 us
    dot_general x8, matrix products, one_block(): jnp.dot(covars_all.T, dose_block, precision=highest, preferred_element_ty...  10.9 us
    another operation x16, other arithmetic, one_block(): beta_dose = jax.scipy.linalg.cho_solve((factor, True), cov_dose)  9.88 us
    unnamed x39, local copies, waits for them, and re-layouts  8.39 us
    all_to_all x1, starting transfers between devices, local(): lax.all_to_all(phenotypes, 'tile', split_axis=1, concat_axis=0, tiled=True)  5.82 us
    dot_general x8, matrix products, one_block(): lax.dot_general(pheno_bf, dose_resid.astype(jnp.bfloat16), (((0,), (0,)),...  4.42 us
  transfers between devices with their start and end apart: 16, of which 14 were waited for; matrix products, arithmetic and copies ran while one was open for 4% of the time, Pallas kernels for 0%

profile of v1, /device:TPU:0, one launch (start us, length us, event | category | flops | bytes accessed | tf_op | source)
XLA Modules:
  0.0 209.9 jit_solution(3852146904921660201)
XLA Ops:
  1.2 9.3 %collective-permute-done = bf16[16,8192]{1,0:T(8,128)(2,1)S(1)} collective-permute-done((bf16[16,8192]{1,0:T(8,128)(2,1)}, bf16[16,8192]{1,0:T(8,128)(2,1)S(1)}, u32[]{:S(2)}, u32[]{:S(2)}) %collective-permute-start) | collective-permute-done | bytes 262176 | tf_op jit(solution)/shard_map/ppermute | solution.py:19
  10.4 8.5 %collective-permute-done.1 = bf16[16,8192]{1,0:T(8,128)(2,1)S(1)} collective-permute-done((bf16[16,8192]{1,0:T(8,128)(2,1)S(1)}, bf16[16,8192]{1,0:T(8,128)(2,1)S(1)}, u32[]{:S(2)}, u32[]{:S(2)}) %collective-permute-start.1) | collective-permute-done | bytes 262176 | tf_op jit(solution)/shard_map/ppermute | solution.py:19
  18.9 8.5 %collective-permute-done.2 = bf16[16,8192]{1,0:T(8,128)(2,1)S(1)} collective-permute-done((bf16[16,8192]{1,0:T(8,128)(2,1)S(1)}, bf16[16,8192]{1,0:T(8,128)(2,1)S(1)}, u32[]{:S(2)}, u32[]{:S(2)}) %collective-permute-start.2) | collective-permute-done | bytes 262176 | tf_op jit(solution)/shard_map/ppermute | solution.py:19
  27.4 8.5 %collective-permute-done.3 = bf16[16,8192]{1,0:T(8,128)(2,1)S(1)} collective-permute-done((bf16[16,8192]{1,0:T(8,128)(2,1)S(1)}, bf16[16,8192]{1,0:T(8,128)(2,1)S(1)}, u32[]{:S(2)}, u32[]{:S(2)}) %collective-permute-start.3) | collective-permute-done | bytes 262176 | tf_op jit(solution)/shard_map/ppermute | solution.py:19
  35.9 8.5 %collective-permute-done.4 = bf16[16,8192]{1,0:T(8,128)(2,1)S(1)} collective-permute-done((bf16[16,8192]{1,0:T(8,128)(2,1)S(1)}, bf16[16,8192]{1,0:T(8,128)(2,1)S(1)}, u32[]{:S(2)}, u32[]{:S(2)}) %collective-permute-start.4) | collective-permute-done | bytes 262176 | tf_op jit(solution)/shard_map/ppermute | solution.py:19
  44.4 8.5 %collective-permute-done.5 = bf16[16,8192]{1,0:T(8,128)(2,1)S(1)} collective-permute-done((bf16[16,8192]{1,0:T(8,128)(2,1)S(1)}, bf16[16,8192]{1,0:T(8,128)(2,1)S(1)}, u32[]{:S(2)}, u32[]{:S(2)}) %collective-permute-start.5) | collective-permute-done | bytes 262176 | tf_op jit(solution)/shard_map/ppermute | solution.py:19
  52.9 8.5 %collective-permute-done.6 = bf16[16,8192]{1,0:T(8,128)(2,1)S(1)} collective-permute-done((bf16[16,8192]{1,0:T(8,128)(2,1)S(1)}, bf16[16,8192]{1,0:T(8,128)(2,1)S(1)}, u32[]{:S(2)}, u32[]{:S(2)}) %collective-permute-start.6) | collective-permute-done | bytes 262176 | tf_op jit(solution)/shard_map/ppermute | solution.py:19
  61.4 8.5 %collective-permute-done.7 = bf16[16,8192]{1,0:T(8,128)(2,1)S(1)} collective-permute-done((bf16[16,8192]{1,0:T(8,128)(2,1)S(1)}, bf16[16,8192]{1,0:T(8,128)(2,1)S(1)}, u32[]{:S(2)}, u32[]{:S(2)}) %collective-permute-start.7) | collective-permute-done | bytes 262176 | tf_op jit(solution)/shard_map/ppermute | solution.py:19
  69.9 8.5 %collective-permute-done.8 = bf16[16,8192]{1,0:T(8,128)(2,1)S(1)} collective-permute-done((bf16[16,8192]{1,0:T(8,128)(2,1)S(1)}, bf16[16,8192]{1,0:T(8,128)(2,1)S(1)}, u32[]{:S(2)}, u32[]{:S(2)}) %collective-permute-start.8) | collective-permute-done | bytes 262176 | tf_op jit(solution)/shard_map/ppermute | solution.py:19
  78.4 8.5 %collective-permute-done.9 = bf16[16,8192]{1,0:T(8,128)(2,1)S(1)} collective-permute-done((bf16[16,8192]{1,0:T(8,128)(2,1)S(1)}, bf16[16,8192]{1,0:T(8,128)(2,1)S(1)}, u32[]{:S(2)}, u32[]{:S(2)}) %collective-permute-start.9) | collective-permute-done | bytes 262176 | tf_op jit(solution)/shard_map/ppermute | solution.py:19
  88.6 5.8 %all-to-all-start = ((f32[16,16,112]{2,0,1:T(8,128)}), f32[16,16,112]{2,0,1:T(8,128)S(1)}, u32[]{:S(2)}, u32[]{:S(2)}) async-start(f32[16,16,112]{2,0,1:T(8,128)} %copy.15), calls=%async_computation | async-start | bytes 262144 | tf_op jit(solution)/shard_map/all_to_all | solution.py:23
  94.4 22.3 %all_gather.3 = f32[256,16]{1,0:T(8,128)S(1)} all-gather(f32[16,16]{1,0:T(8,128)} %param.6), channel_id=1, replica_groups=mesh['cohort'=2,'tile'=16] {'tile'}, dimensions={0}, use_global_device_ids=true | all-gather | bytes 17408 | tf_op jit(solution)/shard_map/all_gather | solution.py:16
  119.6 6.1 %collective-permute-done.11 = bf16[16,8192]{1,0:T(8,128)(2,1)} collective-permute-done((bf16[16,8192]{1,0:T(8,128)(2,1)S(1)}, bf16[16,8192]{1,0:T(8,128)(2,1)}, u32[]{:S(2)}, u32[]{:S(2)}) %collective-permute-start.11) | collective-permute-done | bytes 262176 | tf_op jit(solution)/shard_map/ppermute | solution.py:19
  128.1 6.5 %collective-permute-done.12 = bf16[16,8192]{1,0:T(8,128)(2,1)} collective-permute-done((bf16[16,8192]{1,0:T(8,128)(2,1)}, bf16[16,8192]{1,0:T(8,128)(2,1)}, u32[]{:S(2)}, u32[]{:S(2)}) %collective-permute-start.12) | collective-permute-done | bytes 262176 | tf_op jit(solution)/shard_map/ppermute | solution.py:19
  136.3 7.1 %collective-permute-done.13 = bf16[16,8192]{1,0:T(8,128)(2,1)} collective-permute-done((bf16[16,8192]{1,0:T(8,128)(2,1)}, bf16[16,8192]{1,0:T(8,128)(2,1)}, u32[]{:S(2)}, u32[]{:S(2)}) %collective-permute-start.13) | collective-permute-done | bytes 262176 | tf_op jit(solution)/shard_map/ppermute | solution.py:19
  143.9 8.3 %collective-permute-done.14 = bf16[16,8192]{1,0:T(8,128)(2,1)} collective-permute-done((bf16[16,8192]{1,0:T(8,128)(2,1)}, bf16[16,8192]{1,0:T(8,128)(2,1)}, u32[]{:S(2)}, u32[]{:S(2)}) %collective-permute-start.14) | collective-permute-done | bytes 262176 | tf_op jit(solution)/shard_map/ppermute | solution.py:19
  160.7 2.2 %constant_dynamic-slice_fusion = bf16[256,8192]{1,0:T(8,128)(2,1)} fusion(bf16[512,8192]{1,0:T(8,128)(2,1)S(1)} %constant_dynamic-update-slice_fusion, s32[]{:T(128)S(6)} %select_n.28), kind=kLoop, calls=%fused_computation.73 | loop fusion | bytes 8388612 | tf_op jit(solution)/shard_map/jit(_roll_dynamic)/dynamic_slice | solution.py:20
  162.9 46.5 %while.18 = (s32[]{:T(128)}, f32[112]{0:T(128)S(1)}, f32[112]{0:T(128)S(1)}, bf16[256,8192]{1,0:T(8,128)(2,1)}, f32[16,16]{1,0:T(8,128)S(1)}, /*index=5*/f32[256...) while((s32[]{:T(128)}, f32[112]{0:T(128)S(1)}, ...), condition=%wide.region_7.8_spmd.clone, body=%wide.region_3.7_spmd.clone.sunk | while | flops 168249056 | bytes 2605173 | solution.py:64
  166.0 2.1 %multiply_reduce_fusion.3 = (f32[1024]{0:T(1024)S(1)}, bf16[256,1024]{1,0:T(8,128)(2,1)S(1)}) fusion(f32[16,1024]{1,0:T(8,128)S(1)} %fusion.64, f32[256,16]{0,1:T(8,128)S(1)} %get-tuple-element.375, bf16[256,8192]{1,0:T(8,128)(2,1)} %get-tuple-element.373, s32[]{:T(128)S(6)} %select_n.34), kind=kOutput, calls=%fused_computation.5.clone.1 | convolution fusion | flops 51641344 | bytes 1134596 | tf_op jit(solution)/shard_map/while/body/eval_jaxpr/dot_general | solution.py:46
  171.8 2.1 %multiply_reduce_fusion.3 = (f32[1024]{0:T(1024)S(1)}, bf16[256,1024]{1,0:T(8,128)(2,1)S(1)}) fusion(f32[16,1024]{1,0:T(8,128)S(1)} %fusion.64, f32[256,16]{0,1:T(8,128)S(1)} %get-tuple-element.375, bf16[256,8192]{1,0:T(8,128)(2,1)} %get-tuple-element.373, s32[]{:T(128)S(6)} %select_n.34), kind=kOutput, calls=%fused_computation.5.clone.1 | convolution fusion | flops 51641344 | bytes 1134596 | tf_op jit(solution)/shard_map/while/body/eval_jaxpr/dot_general | solution.py:46
  177.6 2.1 %multiply_reduce_fusion.3 = (f32[1024]{0:T(1024)S(1)}, bf16[256,1024]{1,0:T(8,128)(2,1)S(1)}) fusion(f32[16,1024]{1,0:T(8,128)S(1)} %fusion.64, f32[256,16]{0,1:T(8,128)S(1)} %get-tuple-element.375, bf16[256,8192]{1,0:T(8,128)(2,1)} %get-tuple-element.373, s32[]{:T(128)S(6)} %select_n.34), kind=kOutput, calls=%fused_computation.5.clone.1 | convolution fusion | flops 51641344 | bytes 1134596 | tf_op jit(solution)/shard_map/while/body/eval_jaxpr/dot_general | solution.py:46
  183.4 2.1 %multiply_reduce_fusion.3 = (f32[1024]{0:T(1024)S(1)}, bf16[256,1024]{1,0:T(8,128)(2,1)S(1)}) fusion(f32[16,1024]{1,0:T(8,128)S(1)} %fusion.64, f32[256,16]{0,1:T(8,128)S(1)} %get-tuple-element.375, bf16[256,8192]{1,0:T(8,128)(2,1)} %get-tuple-element.373, s32[]{:T(128)S(6)} %select_n.34), kind=kOutput, calls=%fused_computation.5.clone.1 | convolution fusion | flops 51641344 | bytes 1134596 | tf_op jit(solution)/shard_map/while/body/eval_jaxpr/dot_general | solution.py:46
  195.0 2.1 %multiply_reduce_fusion.3 = (f32[1024]{0:T(1024)S(1)}, bf16[256,1024]{1,0:T(8,128)(2,1)S(1)}) fusion(f32[16,1024]{1,0:T(8,128)S(1)} %fusion.64, f32[256,16]{0,1:T(8,128)S(1)} %get-tuple-element.375, bf16[256,8192]{1,0:T(8,128)(2,1)} %get-tuple-element.373, s32[]{:T(128)S(6)} %select_n.34), kind=kOutput, calls=%fused_computation.5.clone.1 | convolution fusion | flops 51641344 | bytes 1134596 | tf_op jit(solution)/shard_map/while/body/eval_jaxpr/dot_general | solution.py:46
  206.7 2.1 %multiply_reduce_fusion.3 = (f32[1024]{0:T(1024)S(1)}, bf16[256,1024]{1,0:T(8,128)(2,1)S(1)}) fusion(f32[16,1024]{1,0:T(8,128)S(1)} %fusion.64, f32[256,16]{0,1:T(8,128)S(1)} %get-tuple-element.375, bf16[256,8192]{1,0:T(8,128)(2,1)} %get-tuple-element.373, s32[]{:T(128)S(6)} %select_n.34), kind=kOutput, calls=%fused_computation.5.clone.1 | convolution fusion | flops 51641344 | bytes 1134596 | tf_op jit(solution)/shard_map/while/body/eval_jaxpr/dot_general | solution.py:46
  (142 shorter events, 51.7 us)
Async XLA Ops:
  0.6 155.8 %copy-start = (bf16[16,8192]{1,0:T(8,128)(2,1)S(1)}, bf16[16,8192]{1,0:T(8,128)(2,1)}, u32[]{:S(2)}) copy-start(bf16[16,8192]{1,0:T(8,128)(2,1)} %param.5) | copy-start | bytes 786436
  0.6 9.8 %collective-permute-start = (bf16[16,8192]{1,0:T(8,128)(2,1)}, bf16[16,8192]{1,0:T(8,128)(2,1)S(1)}, u32[]{:S(2)}, u32[]{:S(2)}) collective-permute-start(bf16[16,8192]{1,0:T(8,128)(2,1)} %param.5), channel_id=1, source_target_pairs={{0,1},{1,2},{2,3},{3,4},{4,5},{5,6},{6,7},{7,8},{8,9},{9,10},{10,1... | collective-permute-start | bytes 786440 | tf_op jit(solution)/shard_map/ppermute | solution.py:19
  10.4 8.5 %collective-permute-start.1 = (bf16[16,8192]{1,0:T(8,128)(2,1)S(1)}, bf16[16,8192]{1,0:T(8,128)(2,1)S(1)}, u32[]{:S(2)}, u32[]{:S(2)}) collective-permute-start(bf16[16,8192]{1,0:T(8,128)(2,1)S(1)} %collective-permute-done), channel_id=1, source_target_pairs={{0,1},{1,2},{2,3},{3,4},{4,5},{5,6},{6,7},{7,8},{8,9},{9,10},{10,1... | collective-permute-start | bytes 786440 | tf_op jit(solution)/shard_map/ppermute | solution.py:19
  18.9 8.5 %collective-permute-start.2 = (bf16[16,8192]{1,0:T(8,128)(2,1)S(1)}, bf16[16,8192]{1,0:T(8,128)(2,1)S(1)}, u32[]{:S(2)}, u32[]{:S(2)}) collective-permute-start(bf16[16,8192]{1,0:T(8,128)(2,1)S(1)} %collective-permute-done.1), channel_id=1, source_target_pairs={{0,1},{1,2},{2,3},{3,4},{4,5},{5,6},{6,7},{7,8},{8,9},{9,10},{10,1... | collective-permute-start | bytes 786440 | tf_op jit(solution)/shard_map/ppermute | solution.py:19
  27.4 8.5 %collective-permute-start.3 = (bf16[16,8192]{1,0:T(8,128)(2,1)S(1)}, bf16[16,8192]{1,0:T(8,128)(2,1)S(1)}, u32[]{:S(2)}, u32[]{:S(2)}) collective-permute-start(bf16[16,8192]{1,0:T(8,128)(2,1)S(1)} %collective-permute-done.2), channel_id=1, source_target_pairs={{0,1},{1,2},{2,3},{3,4},{4,5},{5,6},{6,7},{7,8},{8,9},{9,10},{10,1... | collective-permute-start | bytes 786440 | tf_op jit(solution)/shard_map/ppermute | solution.py:19
  35.9 8.5 %collective-permute-start.4 = (bf16[16,8192]{1,0:T(8,128)(2,1)S(1)}, bf16[16,8192]{1,0:T(8,128)(2,1)S(1)}, u32[]{:S(2)}, u32[]{:S(2)}) collective-permute-start(bf16[16,8192]{1,0:T(8,128)(2,1)S(1)} %collective-permute-done.3), channel_id=1, source_target_pairs={{0,1},{1,2},{2,3},{3,4},{4,5},{5,6},{6,7},{7,8},{8,9},{9,10},{10,1... | collective-permute-start | bytes 786440 | tf_op jit(solution)/shard_map/ppermute | solution.py:19
  44.4 8.5 %collective-permute-start.5 = (bf16[16,8192]{1,0:T(8,128)(2,1)S(1)}, bf16[16,8192]{1,0:T(8,128)(2,1)S(1)}, u32[]{:S(2)}, u32[]{:S(2)}) collective-permute-start(bf16[16,8192]{1,0:T(8,128)(2,1)S(1)} %collective-permute-done.4), channel_id=1, source_target_pairs={{0,1},{1,2},{2,3},{3,4},{4,5},{5,6},{6,7},{7,8},{8,9},{9,10},{10,1... | collective-permute-start | bytes 786440 | tf_op jit(solution)/shard_map/ppermute | solution.py:19
  52.9 8.5 %collective-permute-start.6 = (bf16[16,8192]{1,0:T(8,128)(2,1)S(1)}, bf16[16,8192]{1,0:T(8,128)(2,1)S(1)}, u32[]{:S(2)}, u32[]{:S(2)}) collective-permute-start(bf16[16,8192]{1,0:T(8,128)(2,1)S(1)} %collective-permute-done.5), channel_id=1, source_target_pairs={{0,1},{1,2},{2,3},{3,4},{4,5},{5,6},{6,7},{7,8},{8,9},{9,10},{10,1... | collective-permute-start | bytes 786440 | tf_op jit(solution)/shard_map/ppermute | solution.py:19
  61.4 8.5 %collective-permute-start.7 = (bf16[16,8192]{1,0:T(8,128)(2,1)S(1)}, bf16[16,8192]{1,0:T(8,128)(2,1)S(1)}, u32[]{:S(2)}, u32[]{:S(2)}) collective-permute-start(bf16[16,8192]{1,0:T(8,128)(2,1)S(1)} %collective-permute-done.6), channel_id=1, source_target_pairs={{0,1},{1,2},{2,3},{3,4},{4,5},{5,6},{6,7},{7,8},{8,9},{9,10},{10,1... | collective-permute-start | bytes 786440 | tf_op jit(solution)/shard_map/ppermute | solution.py:19
  69.9 8.5 %collective-permute-start.8 = (bf16[16,8192]{1,0:T(8,128)(2,1)S(1)}, bf16[16,8192]{1,0:T(8,128)(2,1)S(1)}, u32[]{:S(2)}, u32[]{:S(2)}) collective-permute-start(bf16[16,8192]{1,0:T(8,128)(2,1)S(1)} %collective-permute-done.7), channel_id=1, source_target_pairs={{0,1},{1,2},{2,3},{3,4},{4,5},{5,6},{6,7},{7,8},{8,9},{9,10},{10,1... | collective-permute-start | bytes 786440 | tf_op jit(solution)/shard_map/ppermute | solution.py:19
  78.4 8.5 %collective-permute-start.9 = (bf16[16,8192]{1,0:T(8,128)(2,1)S(1)}, bf16[16,8192]{1,0:T(8,128)(2,1)S(1)}, u32[]{:S(2)}, u32[]{:S(2)}) collective-permute-start(bf16[16,8192]{1,0:T(8,128)(2,1)S(1)} %collective-permute-done.8), channel_id=1, source_target_pairs={{0,1},{1,2},{2,3},{3,4},{4,5},{5,6},{6,7},{7,8},{8,9},{9,10},{10,1... | collective-permute-start | bytes 786440 | tf_op jit(solution)/shard_map/ppermute | solution.py:19
  86.9 30.2 %collective-permute-start.10 = (bf16[16,8192]{1,0:T(8,128)(2,1)S(1)}, bf16[16,8192]{1,0:T(8,128)(2,1)S(1)}, u32[]{:S(2)}, u32[]{:S(2)}) collective-permute-start(bf16[16,8192]{1,0:T(8,128)(2,1)S(1)} %collective-permute-done.9), channel_id=1, source_target_pairs={{0,1},{1,2},{2,3},{3,4},{4,5},{5,6},{6,7},{7,8},{8,9},{9,10},{10,1... | collective-permute-start | bytes 786440 | tf_op jit(solution)/shard_map/ppermute | solution.py:19
  88.6 39.1 %all-to-all-start = ((f32[16,16,112]{2,0,1:T(8,128)}), f32[16,16,112]{2,0,1:T(8,128)S(1)}, u32[]{:S(2)}, u32[]{:S(2)}) async-start(f32[16,16,112]{2,0,1:T(8,128)} %copy.15), calls=%async_computation | async-start | bytes 262144 | tf_op jit(solution)/shard_map/all_to_all | solution.py:23
  117.1 8.6 %collective-permute-start.11 = (bf16[16,8192]{1,0:T(8,128)(2,1)S(1)}, bf16[16,8192]{1,0:T(8,128)(2,1)}, u32[]{:S(2)}, u32[]{:S(2)}) collective-permute-start(bf16[16,8192]{1,0:T(8,128)(2,1)S(1)} %collective-permute-done.10), channel_id=1, source_target_pairs={{0,1},{1,2},{2,3},{3,4},{4,5},{5,6},{6,7},{7,8},{8,9},{9,10},{10,1... | collective-permute-start | bytes 786440 | tf_op jit(solution)/shard_map/ppermute | solution.py:19
  125.8 8.8 %collective-permute-start.12 = (bf16[16,8192]{1,0:T(8,128)(2,1)}, bf16[16,8192]{1,0:T(8,128)(2,1)}, u32[]{:S(2)}, u32[]{:S(2)}) collective-permute-start(bf16[16,8192]{1,0:T(8,128)(2,1)} %collective-permute-done.11), channel_id=1, source_target_pairs={{0,1},{1,2},{2,3},{3,4},{4,5},{5,6},{6,7},{7,8},{8,9},{9,10},{10,1... | collective-permute-start | bytes 786440 | tf_op jit(solution)/shard_map/ppermute | solution.py:19
  134.6 8.8 %collective-permute-start.13 = (bf16[16,8192]{1,0:T(8,128)(2,1)}, bf16[16,8192]{1,0:T(8,128)(2,1)}, u32[]{:S(2)}, u32[]{:S(2)}) collective-permute-start(bf16[16,8192]{1,0:T(8,128)(2,1)} %collective-permute-done.12), channel_id=1, source_target_pairs={{0,1},{1,2},{2,3},{3,4},{4,5},{5,6},{6,7},{7,8},{8,9},{9,10},{10,1... | collective-permute-start | bytes 786440 | tf_op jit(solution)/shard_map/ppermute | solution.py:19
  143.4 8.8 %collective-permute-start.14 = (bf16[16,8192]{1,0:T(8,128)(2,1)}, bf16[16,8192]{1,0:T(8,128)(2,1)}, u32[]{:S(2)}, u32[]{:S(2)}) collective-permute-start(bf16[16,8192]{1,0:T(8,128)(2,1)} %collective-permute-done.13), channel_id=1, source_target_pairs={{0,1},{1,2},{2,3},{3,4},{4,5},{5,6},{6,7},{7,8},{8,9},{9,10},{10,1... | collective-permute-start | bytes 786440 | tf_op jit(solution)/shard_map/ppermute | solution.py:19
  156.4 6.5 %copy-start.1 = (f32[112]{0:T(128)S(1)}, f32[112]{0:T(128)}, u32[]{:S(2)}) copy-start(f32[112]{0:T(128)} %custom-call.25) | copy-start | bytes 1348
  156.4 6.5 %copy-start.2 = (f32[112]{0:T(128)S(1)}, f32[112]{0:T(128)}, u32[]{:S(2)}) copy-start(f32[112]{0:T(128)} %custom-call.26) | copy-start | bytes 1348
